TPU v7x, 32 devices: a whole 2x2x4 slice. The times are simulated.
32 devices in a mesh: groups: 2 (over x), blk: 16 (over z, y, core).
Axes of the slice: x: 2, y: 2, z: 4, core: 2. Of those that a mesh axis runs over, the one named last changes fastest.
Arguments:
- embeddings: bfloat16 [12288, 512], P(('groups', 'blk')), parts along dimension 0, may hold values from -24 to 24
- cluster_ids: int32 [12288], P(('groups', 'blk')), parts along dimension 0, may hold values from 0 to 63, as said below
- cluster_sizes: int32 [128], P('groups'), parts along dimension 0, may hold values from 12 to 960, as said below
Outputs:
- log_density: float32 [12288], P(('groups', 'blk')), parts along dimension 0
- centrality: float32 [12288], P(('groups', 'blk')), parts along dimension 0
There are 2 independent parts, one for each index of `groups`. A program takes and returns all parts, laid end to end along the dimension named above; each array names one. Nothing has to cross between parts.
Inputs may be any that keep to these rules, and one draw needn't show every extreme that they name: cluster_sizes[c] is the number of rows whose cluster id is c; the sizes sum to 6144 and the largest is exactly 960. `cluster_ids`: rows are dealt to the devices of blk: with n the number of devices of blk and E_c the sum of cluster_sizes[c'] mod n over the clusters c' < c, device s holds cluster_sizes[c] // n rows of cluster c, plus one more exactly when (s - E_c) mod n < cluster_sizes[c] mod n. Within a device the rows stand in no particular order.
All inputs are finite; a program needn't handle non-finite values.
Results may differ from a plain program's by a relative error of at most 0.00065.
The roundings to bfloat16 on the way count: a program that leaves them out, or rounds other values in their place, can miss the bound.
Values may be sent and summed in bfloat16 or wider, within the bound.
No kernel may reach another device: no remote copies, remote signals or barrier semaphores. Data moves between devices by JAX's collectives and lax.ppermute only.
A program may use at most 64 MiB of HBM per device.

v0:
```python
import jax
import jax.numpy as jnp
from jax import lax
from jax.sharding import PartitionSpec as P

SOFTMAX_TEMP = 0.1
EPSILON = 1e-06


def shifted(array, axis, by):
    peers = lax.axis_size(axis)
    pairs = [(i, i + by) for i in range(peers) if 0 <= i + by < peers]
    return lax.ppermute(array, axis, pairs)


def unit_rows(embeddings):
    values = embeddings.astype(jnp.float32)
    scale = lax.rsqrt(jnp.mean(values * values, axis=1, keepdims=True) + EPSILON)
    return (values * (scale * values.shape[1] ** (-0.5))).astype(jnp.bfloat16)


def block_terms(remaining_rows, left_labels, right_rows, right_labels):
    similarity_scores = jnp.einsum(
        "rd,kd->rk", remaining_rows, right_rows, preferred_element_type=jnp.float32
    )
    same_cluster = left_labels[:, None] == right_labels[None, :]
    return jnp.sum(jnp.where(same_cluster, jnp.exp(similarity_scores / SOFTMAX_TEMP), 0.0), axis=1)


def lookup(table, one_hot):
    return jnp.sum(jnp.where(one_hot, table[None, :], 0), axis=1)


def sorted_density(unit, cluster_sizes, member):
    devices = lax.axis_size("blk")
    own_index = lax.axis_index("blk")
    rows_dev = unit.shape[0]
    clusters = cluster_sizes.shape[0]
    total_rows = rows_dev * devices
    fewest = total_rows // 512
    largest = total_rows * 5 // 32
    capacity = min(rows_dev, rows_dev // devices + rows_dev // fewest + 2)
    reach = (largest + rows_dev - 2) // rows_dev
    ends = jnp.cumsum(cluster_sizes)
    starts = ends - cluster_sizes
    base = cluster_sizes // devices
    extra = cluster_sizes % devices
    first = (jnp.cumsum(extra) - extra) % devices
    source_rows = jnp.arange(devices, dtype=jnp.int32)
    holds = base[None, :] + (
        (source_rows[:, None] - first[None, :]) % devices < extra[None, :]
    ).astype(jnp.int32)
    member_count = jnp.cumsum(member.astype(jnp.int32), axis=0)
    rank = jnp.sum(jnp.where(member, member_count - 1, 0), axis=1)
    held_row = jnp.dot(
        member.astype(jnp.float32), holds.T.astype(jnp.float32), precision=lax.Precision.HIGHEST
    ).astype(jnp.int32)
    before_me = (source_rows[None, :] < own_index) & (held_row > rank[:, None])
    within = jnp.sum(jnp.minimum(held_row, rank[:, None]), axis=1) + jnp.sum(
        before_me.astype(jnp.int32), axis=1
    )
    position = lookup(starts, member) + within
    target = position // rows_dev
    earlier = (target[None, :] == target[:, None]) & (position[None, :] < position[:, None])
    slot = jnp.sum(earlier.astype(jnp.int32), axis=1)
    address = target * capacity + slot
    sender = (
        jnp.zeros((devices * capacity,), jnp.int32)
        .at[address]
        .set(jnp.arange(rows_dev, dtype=jnp.int32))
    )
    filled = jnp.zeros((devices * capacity,), jnp.bool_).at[address].set(True)
    packed = jnp.where(filled[:, None], unit[sender], jnp.zeros((), jnp.bfloat16))
    arrived = lax.all_to_all(packed, "blk", split_axis=0, concat_axis=0, tiled=True)
    local = jnp.arange(rows_dev, dtype=jnp.int32)
    places = own_index * rows_dev + local
    home_label = jnp.sum((places[:, None] >= ends[None, :]).astype(jnp.int32), axis=1)
    home_cluster_member = home_label[:, None] == jnp.arange(clusters, dtype=jnp.int32)[None, :]
    offset_in = places - lookup(starts, home_cluster_member)
    base_row = lookup(base, home_cluster_member)
    extra_row = lookup(extra, home_cluster_member)
    first_row = lookup(first, home_cluster_member)
    full_rounds = devices * base_row
    surplus = offset_in - full_rounds
    wrapped = first_row + extra_row - devices
    late_source = jnp.where(
        wrapped > 0,
        jnp.where(surplus < wrapped, surplus, first_row + surplus - wrapped),
        first_row + surplus,
    )
    anchor = jnp.where(offset_in < full_rounds, offset_in % devices, late_source)
    anchor_hot = anchor[:, None] == source_rows[None, :]
    anchor_count = jnp.cumsum(anchor_hot.astype(jnp.int32), axis=0)
    order_in = jnp.sum(jnp.where(anchor_hot, anchor_count - 1, 0), axis=1)
    block = arrived[anchor * capacity + order_in]

    def labels_at(spots):
        inside = (spots >= 0) & (spots < total_rows)
        found = jnp.sum((spots[:, None] >= ends[None, :]).astype(jnp.int32), axis=1)
        return jnp.where(inside, found, -1)

    density = block_terms(block, home_label, block, home_label)

    def advance(offset, carried_rows):
        upper, lower, running = carried_rows
        upper = shifted(upper, "blk", 1)
        lower = shifted(lower, "blk", -1)
        running = running + block_terms(
            block, home_label, upper, labels_at(places - offset * rows_dev)
        )
        running = running + block_terms(
            block, home_label, lower, labels_at(places + offset * rows_dev)
        )
        return (upper, lower, running)

    carried_out = lax.fori_loop(1, reach + 1, advance, (block, block, density))
    density = carried_out[2]
    returned = (
        jnp.zeros((devices * capacity,), jnp.float32).at[anchor * capacity + order_in].set(density)
    )
    answered = lax.all_to_all(returned, "blk", split_axis=0, concat_axis=0, tiled=True)
    return answered[address]


def on_device(embeddings, cluster_ids, cluster_sizes):
    unit = unit_rows(embeddings)
    clusters = cluster_sizes.shape[0]
    member = cluster_ids[:, None] == jnp.arange(clusters, dtype=jnp.int32)[None, :]
    partial_sum = jnp.einsum(
        "rc,rd->cd", member.astype(jnp.bfloat16), unit, preferred_element_type=jnp.float32
    )
    centroid = lax.psum(partial_sum, "blk")
    density = sorted_density(unit, cluster_sizes, member)
    sizes_row = lookup(cluster_sizes, member).astype(jnp.float32)
    log_density = jnp.log(density / sizes_row)
    projected = jnp.dot(unit.astype(jnp.float32), centroid.T, precision=lax.Precision.HIGHEST)
    centrality = jnp.sum(jnp.where(member, projected, 0.0), axis=1) / sizes_row
    return (log_density, centrality)


def solution(mesh):
    in_specs = (P(("groups", "blk"), None), P(("groups", "blk")), P("groups"))
    out_specs = (P(("groups", "blk")), P(("groups", "blk")))
    return jax.shard_map(
        on_device, mesh=mesh, in_specs=in_specs, out_specs=out_specs, check_vma=False
    )
```

profile of v0, /device:TPU:8, one launch (start us, length us, event | category | flops | bytes accessed | tf_op | source)
XLA Modules:
  0.0 142.4 jit_solution(12733876175211087510)
XLA Ops:
  7.2 1.2 fusion.14
  8.4 0.1 fusion.15
  8.6 0.0 copy-start.2
  8.6 0.6 copy-done.2
  9.2 0.1 copy.17
  9.3 0.1 reduce-window.37
  9.4 0.1 reduce
  9.5 0.1 copy.18
  9.6 0.1 reduce-window.38
  9.7 0.1 reduce.1
  9.9 0.0 copy-start.1
  9.9 0.1 convert_reduce_fusion.3
  10.0 0.6 copy-done.1
  10.6 0.9 reduce-window.41
  11.5 0.2 slice_reduce_fusion
  11.7 0.2 select_reduce_fusion
  11.9 0.3 convert_reduce_fusion.4
  12.3 0.3 convert_reduce_fusion.2
  12.6 2.9 %scatter_custom_fusion.1 = s32[928]{0:T(1024)S(1)} fusion(s32[384]{0:T(512)S(1)} %fusion.58, s32[384]{0:T(512)S(1)} %iota.57, s32[]{:T(128)} %copy.40), kind=kCustom, calls=%fused_computation.120 | custom fusion | bytes 3716 | tf_op jit(solution)/shard_map/scatter | solution.py:70
  15.5 4.0 %gather_fusion = bf16[928,512]{1,0:T(8,128)(2,1)S(1)} fusion(bf16[384,512]{1,0:T(8,128)(2,1)S(1)} %fusion.15, s32[1024]{0:T(1024)S(1)} %pad_clamp_fusion.2), kind=kCustom, calls=%fused_computation | custom fusion | bytes 1904256 | tf_op jit(solution)/shard_map/gather | solution.py:73
  19.6 0.2 gather.12
  19.8 2.0 %scatter_custom_fusion = pred[928]{0:T(1024)(128)(4,1)S(1)} fusion(s32[384]{0:T(512)S(1)} %fusion.58, pred[384]{0:T(512)(128)(4,1)S(1)} %broadcast.470, pred[]{:T(512)} %constant.152.clone.1), kind=kCustom, calls=%fused_computation.132 | custom fusion | bytes 929 | tf_op jit(solution)/shard_map/scatter | solution.py:72
  21.8 0.1 broadcast_in_dim.158
  21.9 1.2 broadcast_select_fusion
  23.1 6.3 %all-to-all-start = ((bf16[16,58,512]{2,1,0:T(8,128)(2,1)}), bf16[16,58,512]{2,1,0:T(8,128)(2,1)S(1)}, u32[]{:S(2)}, u32[]{:S(2)}) async-start(bf16[16,58,512]{2,1,0:T(8,128)(2,1)} %broadcast_select_fusion), calls=%async_computation | async-start | bytes 2097152 | tf_op jit(solution)/shard_map/all_to_all | solution.py:74
  29.4 0.0 all-reduce.2.cloned.1.call-start
  29.5 0.8 fusion.18
  30.3 0.0 all-reduce.2.cloned.1.call-update
  30.4 0.9 reduce-window.39
  31.2 0.2 slice_reduce_fusion.1
  31.5 0.1 fusion.34
  31.7 22.5 %all-to-all-done = bf16[16,58,512]{2,1,0:T(8,128)(2,1)S(1)} async-done(((bf16[16,58,512]{2,1,0:T(8,128)(2,1)}), bf16[16,58,512]{2,1,0:T(8,128)(2,1)S(1)}, u32[]{:S(2)}, u32[]{:S(2)}) %all-to-all-start) | async-done | bytes 950304 | tf_op jit(solution)/shard_map/all_to_all | solution.py:74
  54.2 0.3 all_to_all.15
  54.4 2.1 %gather_fusion.1 = bf16[384,512]{1,0:T(8,128)(2,1)S(1)} fusion(bf16[928,512]{1,0:T(8,128)(2,1)S(1)} %all_to_all.15, s32[1024]{0:T(1024)S(1)} %pad_clamp_fusion.1), kind=kCustom, calls=%fused_computation.1 | custom fusion | bytes 787968 | tf_op jit(solution)/shard_map/gather | solution.py:95
  56.6 0.4 fusion.12
  57.0 38.6 %while.18 = (s32[]{:T(128)}, bf16[384,512]{1,0:T(8,128)(2,1)S(1)}, bf16[384,512]{1,0:T(8,128)(2,1)S(1)}, f32[384]{0:T(512)S(1)}, s32[384]{0:T(512)S(1)}, /*index...) while((s32[]{:T(128)}, bf16[384,512]{1,0:T(8,128)(2,1)S(1)}, ...), condition=%wide.region_26.27_spmd.clone, body=%wide.region_21.26_spmd.clone.sunk | while | flops 303321984 | bytes 6322649 | solution.py:116
  57.0 2.9 %collective-permute-start = (bf16[384,512]{1,0:T(8,128)(2,1)S(1)}, bf16[384,512]{1,0:T(8,128)(2,1)S(1)}, u32[]{:S(2)}, u32[]{:S(2)}) collective-permute-start(bf16[384,512]{1,0:T(8,128)(2,1)S(1)} %get-tuple-element.275), channel_id=1, source_target_pairs={{0,1},{1,2},{2,3},{3,4},{4,5},{5,6},{6,7},{7,8},{8,9},{9,10},{10,1... | collective-permute-start | bytes 1179656 | tf_op jit(solution)/shard_map/while/body/eval_jaxpr/ppermute | solution.py:13
  59.9 3.5 %collective-permute-start.1 = (bf16[384,512]{1,0:T(8,128)(2,1)S(1)}, bf16[384,512]{1,0:T(8,128)(2,1)S(1)}, u32[]{:S(2)}, u32[]{:S(2)}) collective-permute-start(bf16[384,512]{1,0:T(8,128)(2,1)S(1)} %get-tuple-element.276), channel_id=1, source_target_pairs={{1,0},{2,1},{3,2},{4,3},{5,4},{6,5},{7,6},{8,7},{9,8},{10,9},{11,1... | collective-permute-start | bytes 1179656 | tf_op jit(solution)/shard_map/while/body/eval_jaxpr/ppermute | solution.py:13
  63.5 0.1 convert_reduce_fusion.6
  63.6 5.1 %collective-permute-done.1 = bf16[384,512]{1,0:T(8,128)(2,1)S(1)} collective-permute-done((bf16[384,512]{1,0:T(8,128)(2,1)S(1)}, bf16[384,512]{1,0:T(8,128)(2,1)S(1)}, u32[]{:S(2)}, u32[]{:S(2)}) %collective-permute-start.1) | collective-permute-done | bytes 393248 | tf_op jit(solution)/shard_map/while/body/eval_jaxpr/ppermute | solution.py:13
  68.7 0.4 fusion.89
  69.2 0.4 fusion.90
  69.7 4.3 %collective-permute-start = (bf16[384,512]{1,0:T(8,128)(2,1)S(1)}, bf16[384,512]{1,0:T(8,128)(2,1)S(1)}, u32[]{:S(2)}, u32[]{:S(2)}) collective-permute-start(bf16[384,512]{1,0:T(8,128)(2,1)S(1)} %get-tuple-element.275), channel_id=1, source_target_pairs={{0,1},{1,2},{2,3},{3,4},{4,5},{5,6},{6,7},{7,8},{8,9},{9,10},{10,1... | collective-permute-start | bytes 1179656 | tf_op jit(solution)/shard_map/while/body/eval_jaxpr/ppermute | solution.py:13
  74.0 2.3 %collective-permute-start.1 = (bf16[384,512]{1,0:T(8,128)(2,1)S(1)}, bf16[384,512]{1,0:T(8,128)(2,1)S(1)}, u32[]{:S(2)}, u32[]{:S(2)}) collective-permute-start(bf16[384,512]{1,0:T(8,128)(2,1)S(1)} %get-tuple-element.276), channel_id=1, source_target_pairs={{1,0},{2,1},{3,2},{4,3},{5,4},{6,5},{7,6},{8,7},{9,8},{10,9},{11,1... | collective-permute-start | bytes 1179656 | tf_op jit(solution)/shard_map/while/body/eval_jaxpr/ppermute | solution.py:13
  76.3 0.1 convert_reduce_fusion.6
  76.5 5.2 %collective-permute-done.1 = bf16[384,512]{1,0:T(8,128)(2,1)S(1)} collective-permute-done((bf16[384,512]{1,0:T(8,128)(2,1)S(1)}, bf16[384,512]{1,0:T(8,128)(2,1)S(1)}, u32[]{:S(2)}, u32[]{:S(2)}) %collective-permute-start.1) | collective-permute-done | bytes 393248 | tf_op jit(solution)/shard_map/while/body/eval_jaxpr/ppermute | solution.py:13
  81.7 0.4 fusion.89
  82.1 0.4 fusion.90
  82.6 4.2 %collective-permute-start = (bf16[384,512]{1,0:T(8,128)(2,1)S(1)}, bf16[384,512]{1,0:T(8,128)(2,1)S(1)}, u32[]{:S(2)}, u32[]{:S(2)}) collective-permute-start(bf16[384,512]{1,0:T(8,128)(2,1)S(1)} %get-tuple-element.275), channel_id=1, source_target_pairs={{0,1},{1,2},{2,3},{3,4},{4,5},{5,6},{6,7},{7,8},{8,9},{9,10},{10,1... | collective-permute-start | bytes 1179656 | tf_op jit(solution)/shard_map/while/body/eval_jaxpr/ppermute | solution.py:13
  86.8 2.4 %collective-permute-start.1 = (bf16[384,512]{1,0:T(8,128)(2,1)S(1)}, bf16[384,512]{1,0:T(8,128)(2,1)S(1)}, u32[]{:S(2)}, u32[]{:S(2)}) collective-permute-start(bf16[384,512]{1,0:T(8,128)(2,1)S(1)} %get-tuple-element.276), channel_id=1, source_target_pairs={{1,0},{2,1},{3,2},{4,3},{5,4},{6,5},{7,6},{8,7},{9,8},{10,9},{11,1... | collective-permute-start | bytes 1179656 | tf_op jit(solution)/shard_map/while/body/eval_jaxpr/ppermute | solution.py:13
  89.3 0.1 convert_reduce_fusion.6
  89.4 5.2 %collective-permute-done.1 = bf16[384,512]{1,0:T(8,128)(2,1)S(1)} collective-permute-done((bf16[384,512]{1,0:T(8,128)(2,1)S(1)}, bf16[384,512]{1,0:T(8,128)(2,1)S(1)}, u32[]{:S(2)}, u32[]{:S(2)}) %collective-permute-start.1) | collective-permute-done | bytes 393248 | tf_op jit(solution)/shard_map/while/body/eval_jaxpr/ppermute | solution.py:13
  94.6 0.4 fusion.89
  95.0 0.4 fusion.90
  95.5 2.9 %scatter_custom_fusion.2 = f32[928]{0:T(1024)S(1)} fusion(s32[384]{0:T(512)S(1)} %fusion.57, f32[384]{0:T(512)S(1)} %get-tuple-element.141, f32[]{:T(128)} %constant.139.clone.1), kind=kCustom, calls=%fused_computation.128 | custom fusion | bytes 3716 | tf_op jit(solution)/shard_map/scatter | solution.py:119
  98.5 0.7 all_to_all.16
  99.1 8.8 %all-to-all-start.1 = ((f32[16,58,1]{1,2,0:T(1,128)}), f32[16,58,1]{1,2,0:T(1,128)S(1)}, u32[]{:S(2)}, u32[]{:S(2)}) async-start(f32[16,58,1]{1,2,0:T(1,128)} %bitcast.9), calls=%async_computation.1 | async-start | bytes 16384 | tf_op jit(solution)/shard_map/all_to_all | solution.py:121
  107.9 22.5 %all-reduce.2.cloned.1.call-done = f32[64,512]{1,0:T(8,128)} async-done(((f32[64,512]{1,0:T(8,128)}), f32[64,512]{1,0:T(8,128)}) %all-reduce.2.cloned.1.call-update) | async-done | bytes 131088 | tf_op jit(solution)/shard_map/psum | solution.py:132
  130.4 1.4 fusion.13
  131.8 0.5 broadcast.549
  132.3 0.7 reduce.13
  133.0 0.1 all_to_all.18
  133.0 1.9 %gather_fusion.2 = f32[384]{0:T(512)S(1)} fusion(f32[928]{0:T(1024)S(1)} %all_to_all.18, s32[1024]{0:T(1024)S(1)} %pad_clamp_fusion), kind=kCustom, calls=%fused_computation.2 | custom fusion | bytes 4608 | tf_op jit(solution)/shard_map/gather | solution.py:122
  134.9 0.6 convert_divide_fusion
  (46 shorter events, 0.6 us)
Async XLA Ops:
  7.2 1.2 copy-start
  8.6 0.7 copy-start.2
  9.9 0.7 copy-start.1
  23.1 31.0 %all-to-all-start = ((bf16[16,58,512]{2,1,0:T(8,128)(2,1)}), bf16[16,58,512]{2,1,0:T(8,128)(2,1)S(1)}, u32[]{:S(2)}, u32[]{:S(2)}) async-start(bf16[16,58,512]{2,1,0:T(8,128)(2,1)} %broadcast_select_fusion), calls=%async_computation | async-start | bytes 2097152 | tf_op jit(solution)/shard_map/all_to_all | solution.py:74
  29.4 101.0 %all-reduce.2.cloned.1.call-start = ((), (), s32[]{:S(2)}) async-start(), calls=%async_computation.2 | async-start | bytes 262144 | tf_op jit(solution)/shard_map/psum | solution.py:132
  57.0 12.2 %collective-permute-start = (bf16[384,512]{1,0:T(8,128)(2,1)S(1)}, bf16[384,512]{1,0:T(8,128)(2,1)S(1)}, u32[]{:S(2)}, u32[]{:S(2)}) collective-permute-start(bf16[384,512]{1,0:T(8,128)(2,1)S(1)} %get-tuple-element.275), channel_id=1, source_target_pairs={{0,1},{1,2},{2,3},{3,4},{4,5},{5,6},{6,7},{7,8},{8,9},{9,10},{10,1... | collective-permute-start | bytes 1179656 | tf_op jit(solution)/shard_map/while/body/eval_jaxpr/ppermute | solution.py:13
  59.9 8.8 %collective-permute-start.1 = (bf16[384,512]{1,0:T(8,128)(2,1)S(1)}, bf16[384,512]{1,0:T(8,128)(2,1)S(1)}, u32[]{:S(2)}, u32[]{:S(2)}) collective-permute-start(bf16[384,512]{1,0:T(8,128)(2,1)S(1)} %get-tuple-element.276), channel_id=1, source_target_pairs={{1,0},{2,1},{3,2},{4,3},{5,4},{6,5},{7,6},{8,7},{9,8},{10,9},{11,1... | collective-permute-start | bytes 1179656 | tf_op jit(solution)/shard_map/while/body/eval_jaxpr/ppermute | solution.py:13
  69.7 12.4 %collective-permute-start = (bf16[384,512]{1,0:T(8,128)(2,1)S(1)}, bf16[384,512]{1,0:T(8,128)(2,1)S(1)}, u32[]{:S(2)}, u32[]{:S(2)}) collective-permute-start(bf16[384,512]{1,0:T(8,128)(2,1)S(1)} %get-tuple-element.275), channel_id=1, source_target_pairs={{0,1},{1,2},{2,3},{3,4},{4,5},{5,6},{6,7},{7,8},{8,9},{9,10},{10,1... | collective-permute-start | bytes 1179656 | tf_op jit(solution)/shard_map/while/body/eval_jaxpr/ppermute | solution.py:13
  74.0 7.7 %collective-permute-start.1 = (bf16[384,512]{1,0:T(8,128)(2,1)S(1)}, bf16[384,512]{1,0:T(8,128)(2,1)S(1)}, u32[]{:S(2)}, u32[]{:S(2)}) collective-permute-start(bf16[384,512]{1,0:T(8,128)(2,1)S(1)} %get-tuple-element.276), channel_id=1, source_target_pairs={{1,0},{2,1},{3,2},{4,3},{5,4},{6,5},{7,6},{8,7},{9,8},{10,9},{11,1... | collective-permute-start | bytes 1179656 | tf_op jit(solution)/shard_map/while/body/eval_jaxpr/ppermute | solution.py:13
  82.6 12.4 %collective-permute-start = (bf16[384,512]{1,0:T(8,128)(2,1)S(1)}, bf16[384,512]{1,0:T(8,128)(2,1)S(1)}, u32[]{:S(2)}, u32[]{:S(2)}) collective-permute-start(bf16[384,512]{1,0:T(8,128)(2,1)S(1)} %get-tuple-element.275), channel_id=1, source_target_pairs={{0,1},{1,2},{2,3},{3,4},{4,5},{5,6},{6,7},{7,8},{8,9},{9,10},{10,1... | collective-permute-start | bytes 1179656 | tf_op jit(solution)/shard_map/while/body/eval_jaxpr/ppermute | solution.py:13
  86.8 7.7 %collective-permute-start.1 = (bf16[384,512]{1,0:T(8,128)(2,1)S(1)}, bf16[384,512]{1,0:T(8,128)(2,1)S(1)}, u32[]{:S(2)}, u32[]{:S(2)}) collective-permute-start(bf16[384,512]{1,0:T(8,128)(2,1)S(1)} %get-tuple-element.276), channel_id=1, source_target_pairs={{1,0},{2,1},{3,2},{4,3},{5,4},{6,5},{7,6},{8,7},{9,8},{10,9},{11,1... | collective-permute-start | bytes 1179656 | tf_op jit(solution)/shard_map/while/body/eval_jaxpr/ppermute | solution.py:13
  99.1 32.6 %all-to-all-start.1 = ((f32[16,58,1]{1,2,0:T(1,128)}), f32[16,58,1]{1,2,0:T(1,128)S(1)}, u32[]{:S(2)}, u32[]{:S(2)}) async-start(f32[16,58,1]{1,2,0:T(1,128)} %bitcast.9), calls=%async_computation.1 | async-start | bytes 16384 | tf_op jit(solution)/shard_map/all_to_all | solution.py:121
Sparse Core Ops, SparseCore 0:
  33.7 96.6 all-reduce.1
where the time goes:
time: 143 us; the launch traced here: 142 us
  waiting for transfers between devices  60.5 us (42%)
  starting transfers between devices  34.8 us (24%)
  local copies, waits for them, and re-layouts  19.8 us (14%)
  between operations  14.3 us (10%)
  other arithmetic  7.29 us (5%)
  matrix products  5.41 us (4%)
    all_to_all x1, waiting for transfers between devices, sorted_density(): lax.all_to_all(packed, 'blk', split_axis=0, concat_axis=0, tiled=True)  22.5 us
    psum x1, waiting for transfers between devices, on_device(): centroid = lax.psum(partial_sum, 'blk')  22.5 us
    ppermute x6, starting transfers between devices, shifted(): return lax.ppermute(array, axis, pairs)  19.7 us
    ppermute x6, waiting for transfers between devices, shifted(): return lax.ppermute(array, axis, pairs)  15.5 us
    all_to_all x1, starting transfers between devices, sorted_density(): lax.all_to_all(returned, 'blk', split_axis=0, concat_axis=0, tiled=True)  8.78 us
    all_to_all x1, starting transfers between devices, sorted_density(): lax.all_to_all(packed, 'blk', split_axis=0, concat_axis=0, tiled=True)  6.3 us
    gather x2, local copies, waits for them, and re-layouts, sorted_density(): unit[sender]  4.29 us
    scatter x1, local copies, waits for them, and re-layouts, sorted_density(): sender = jnp.zeros((devices * capacity,), jnp.int32).at[address].set(jnp....  2.92 us
  transfers between devices with their start and end apart: 9, of which 5 were waited for; matrix products, arithmetic and copies ran while one was open for 8% of the time, Pallas kernels for 0%

commit v1 on v0

--- a/solution.py
+++ b/solution.py
@@ -5,6 +5,21 @@
 
 SOFTMAX_TEMP = 0.1
 EPSILON = 1e-06
+
+
+def end_the_tasks(incoming_x, array_dim, own_rows):
+    r1, step_out = (incoming_x.shape[:array_dim], incoming_x.shape[array_dim + 1 :])
+    state_now = jnp.moveaxis(incoming_x.reshape(*r1, own_rows, -1, *step_out), array_dim, 0)
+    return state_now
+
+
+def advance_the_series(block_in, d_out):
+    block_in = jnp.moveaxis(block_in, 0, d_out)
+    x_now = block_in.shape
+    current_arr = block_in.reshape(
+        *x_now[:d_out], x_now[d_out] * x_now[d_out + 1], *x_now[d_out + 2 :]
+    )
+    return current_arr
 
 
 def shifted(array, axis, by):
@@ -32,6 +47,22 @@
 
 
 def sorted_density(unit, cluster_sizes, member):
+
+    def array_state(xin, comm_axis, my_data, payload):
+        new = lax.axis_size(comm_axis)
+        o_now, current_block = (new, lax.axis_index(comm_axis))
+        all_rows = end_the_tasks(xin, my_data, o_now)
+        cards = [all_rows[current_block]]
+        for pp in [*range(1, o_now)]:
+            then = all_rows[current_block ^ pp]
+            piece_out = lax.ppermute(
+                then, axis_name=comm_axis, perm=[(t, t ^ pp) for t in range(o_now)]
+            )
+            cards.append(piece_out)
+        all_rows = jnp.stack(cards, axis=0)[current_block ^ jnp.arange(o_now)]
+        y2 = advance_the_series(all_rows, payload)
+        return y2
+
     devices = lax.axis_size("blk")
     own_index = lax.axis_index("blk")
     rows_dev = unit.shape[0]
@@ -71,7 +102,7 @@
     )
     filled = jnp.zeros((devices * capacity,), jnp.bool_).at[address].set(True)
     packed = jnp.where(filled[:, None], unit[sender], jnp.zeros((), jnp.bfloat16))
-    arrived = lax.all_to_all(packed, "blk", split_axis=0, concat_axis=0, tiled=True)
+    arrived = array_state(packed, "blk", 0, 0)
     local = jnp.arange(rows_dev, dtype=jnp.int32)
     places = own_index * rows_dev + local
     home_label = jnp.sum((places[:, None] >= ends[None, :]).astype(jnp.int32), axis=1)

time: 143 us -> 131 us (0.916)
  the two profiles are of different devices: /device:TPU:8 before, /device:TPU:0 now
where the time goes in v1:
time: 131 us
  starting transfers between devices  65.4 us (50%)
  local copies, waits for them, and re-layouts  20.6 us (16%)
  waiting for transfers between devices  18.3 us (14%)
  between operations  14.6 us (11%)
  other arithmetic  6.29 us (5%)
  matrix products  5.42 us (4%)
    ppermute x15, starting transfers between devices, array_state(): lax.ppermute(then, axis_name=comm_axis, perm=[(t, t ^ pp) for t in range(...  27.2 us
    ppermute x6, starting transfers between devices, shifted(): return lax.ppermute(array, axis, pairs)  24.7 us
    all_to_all x1, starting transfers between devices, sorted_density(): lax.all_to_all(returned, 'blk', split_axis=0, concat_axis=0, tiled=True)  13.4 us
    ppermute x15, waiting for transfers between devices, array_state(): lax.ppermute(then, axis_name=comm_axis, perm=[(t, t ^ pp) for t in range(...  6.71 us
    ppermute x6, waiting for transfers between devices, shifted(): return lax.ppermute(array, axis, pairs)  6.53 us
    all_to_all x1, waiting for transfers between devices, sorted_density(): lax.all_to_all(returned, 'blk', split_axis=0, concat_axis=0, tiled=True)  5.02 us
    gather x2, local copies, waits for them, and re-layouts, sorted_density(): unit[sender]  4.29 us
    scatter x1, local copies, waits for them, and re-layouts, sorted_density(): jnp.zeros((devices * capacity,), jnp.float32)  2.92 us
  transfers between devices with their start and end apart: 23, of which 8 were waited for; matrix products, arithmetic and copies ran while one was open for 19% of the time, Pallas kernels for 0%

profile of v1, /device:TPU:0, one launch (start us, length us, event | category | flops | bytes accessed | tf_op | source)
XLA Modules:
  0.0 130.8 jit_solution(8712553569688075447)
XLA Ops:
  7.2 1.2 fusion.14
  8.4 0.1 fusion.15
  8.6 0.5 copy-done.1
  9.1 0.8 fusion.18
  10.0 0.6 copy-done.2
  11.4 0.9 reduce-window.41
  12.3 0.2 slice_reduce_fusion
  12.6 0.2 select_reduce_fusion
  12.9 0.9 reduce-window.39
  13.8 0.2 slice_reduce_fusion.1
  14.0 0.3 convert_reduce_fusion.4
  14.4 0.3 convert_reduce_fusion.2
  14.7 2.9 %scatter_custom_fusion.1 = s32[928]{0:T(1024)S(1)} fusion(s32[384]{0:T(512)S(1)} %fusion.59, s32[384]{0:T(512)S(1)} %iota.61, s32[]{:T(128)} %copy.55), kind=kCustom, calls=%fused_computation.155 | custom fusion | bytes 3716 | tf_op jit(solution)/shard_map/scatter | solution.py:101
  17.8 4.0 %gather_fusion = bf16[928,512]{1,0:T(8,128)(2,1)S(1)} fusion(bf16[384,512]{1,0:T(8,128)(2,1)S(1)} %fusion.15, s32[1024]{0:T(1024)S(1)} %get-tuple-element.222), kind=kCustom, calls=%fused_computation | custom fusion | bytes 1904256 | tf_op jit(solution)/shard_map/gather | solution.py:104
  21.8 0.2 gather.15
  22.1 2.0 %scatter_custom_fusion = pred[928]{0:T(1024)(128)(4,1)S(1)} fusion(s32[384]{0:T(512)S(1)} %fusion.59, pred[384]{0:T(512)(128)(4,1)S(1)} %broadcast.499, pred[]{:T(512)} %constant.168.clone.1), kind=kCustom, calls=%fused_computation.167 | custom fusion | bytes 929 | tf_op jit(solution)/shard_map/scatter | solution.py:103
  24.2 0.2 broadcast_select_fusion
  24.5 0.2 dynamic-slice_bitcast_fusion
  24.6 0.6 collective-permute-start.2
  25.2 2.6 %collective-permute-start.3 = (bf16[58,512]{1,0:T(8,128)(2,1)S(1)}, bf16[58,512]{1,0:T(8,128)(2,1)S(1)}, u32[]{:S(2)}, u32[]{:S(2)}) collective-permute-start(bf16[58,512]{1,0:T(8,128)(2,1)S(1)} %get-tuple-element.207), channel_id=1, source_target_pairs={{0,2},{1,3},{2,0},{3,1},{4,6},{5,7},{6,4},{7,5},{8,10},{9,11},{10,... | collective-permute-start | bytes 178184 | tf_op jit(solution)/shard_map/ppermute | solution.py:58
  27.8 1.8 %collective-permute-start.5 = (bf16[58,512]{1,0:T(8,128)(2,1)S(1)}, bf16[58,512]{1,0:T(8,128)(2,1)S(1)}, u32[]{:S(2)}, u32[]{:S(2)}) collective-permute-start(bf16[58,512]{1,0:T(8,128)(2,1)S(1)} %get-tuple-element.205), channel_id=1, source_target_pairs={{0,4},{1,5},{2,6},{3,7},{4,0},{5,1},{6,2},{7,3},{8,12},{9,13},{10,... | collective-permute-start | bytes 178184 | tf_op jit(solution)/shard_map/ppermute | solution.py:58
  29.7 2.7 %collective-permute-start.7 = (bf16[58,512]{1,0:T(8,128)(2,1)S(1)}, bf16[58,512]{1,0:T(8,128)(2,1)S(1)}, u32[]{:S(2)}, u32[]{:S(2)}) collective-permute-start(bf16[58,512]{1,0:T(8,128)(2,1)S(1)} %get-tuple-element.203), channel_id=1, source_target_pairs={{0,6},{1,7},{2,4},{3,5},{4,2},{5,3},{6,0},{7,1},{8,14},{9,15},{10,... | collective-permute-start | bytes 178184 | tf_op jit(solution)/shard_map/ppermute | solution.py:58
  32.5 0.1 collective-permute-start.8
  32.6 2.7 %collective-permute-start.9 = (bf16[58,512]{1,0:T(8,128)(2,1)S(1)}, bf16[58,512]{1,0:T(8,128)(2,1)S(1)}, u32[]{:S(2)}, u32[]{:S(2)}) collective-permute-start(bf16[58,512]{1,0:T(8,128)(2,1)S(1)} %get-tuple-element.201), channel_id=1, source_target_pairs={{0,8},{1,9},{2,10},{3,11},{4,12},{5,13},{6,14},{7,15},{8,0},{9,1},... | collective-permute-start | bytes 178184 | tf_op jit(solution)/shard_map/ppermute | solution.py:58
  35.4 1.0 collective-permute-start.10
  36.3 2.7 %collective-permute-start.11 = (bf16[58,512]{1,0:T(8,128)(2,1)S(1)}, bf16[58,512]{1,0:T(8,128)(2,1)S(1)}, u32[]{:S(2)}, u32[]{:S(2)}) collective-permute-start(bf16[58,512]{1,0:T(8,128)(2,1)S(1)} %get-tuple-element.199), channel_id=1, source_target_pairs={{0,10},{1,11},{2,8},{3,9},{4,14},{5,15},{6,12},{7,13},{8,2},{9,3},... | collective-permute-start | bytes 178184 | tf_op jit(solution)/shard_map/ppermute | solution.py:58
  39.1 0.7 collective-permute-start.12
  39.7 3.1 %collective-permute-start.13 = (bf16[58,512]{1,0:T(8,128)(2,1)S(1)}, bf16[58,512]{1,0:T(8,128)(2,1)S(1)}, u32[]{:S(2)}, u32[]{:S(2)}) collective-permute-start(bf16[58,512]{1,0:T(8,128)(2,1)S(1)} %get-tuple-element.197), channel_id=1, source_target_pairs={{0,12},{1,13},{2,14},{3,15},{4,8},{5,9},{6,10},{7,11},{8,4},{9,5},... | collective-permute-start | bytes 178184 | tf_op jit(solution)/shard_map/ppermute | solution.py:58
  42.9 3.8 %collective-permute-start.14 = (bf16[58,512]{1,0:T(8,128)(2,1)S(1)}, bf16[58,512]{1,0:T(8,128)(2,1)S(1)}, u32[]{:S(2)}, u32[]{:S(2)}) collective-permute-start(bf16[58,512]{1,0:T(8,128)(2,1)S(1)} %get-tuple-element.196), channel_id=1, source_target_pairs={{0,13},{1,12},{2,15},{3,14},{4,9},{5,8},{6,11},{7,10},{8,5},{9,4},... | collective-permute-start | bytes 178184 | tf_op jit(solution)/shard_map/ppermute | solution.py:58
  46.6 0.8 collective-permute-done.10
  47.5 3.3 %collective-permute-start.15 = (bf16[58,512]{1,0:T(8,128)(2,1)S(1)}, bf16[58,512]{1,0:T(8,128)(2,1)S(1)}, u32[]{:S(2)}, u32[]{:S(2)}) collective-permute-start(bf16[58,512]{1,0:T(8,128)(2,1)S(1)} %get-tuple-element.195), channel_id=1, source_target_pairs={{0,14},{1,15},{2,12},{3,13},{4,10},{5,11},{6,8},{7,9},{8,6},{9,7},... | collective-permute-start | bytes 178184 | tf_op jit(solution)/shard_map/ppermute | solution.py:58
  50.8 0.8 collective-permute-done.11
  51.6 2.1 %collective-permute-start.16 = (bf16[58,512]{1,0:T(8,128)(2,1)S(1)}, bf16[58,512]{1,0:T(8,128)(2,1)S(1)}, u32[]{:S(2)}, u32[]{:S(2)}) collective-permute-start(bf16[58,512]{1,0:T(8,128)(2,1)S(1)} %get-tuple-element.194), channel_id=1, source_target_pairs={{0,15},{1,14},{2,13},{3,12},{4,11},{5,10},{6,9},{7,8},{8,7},{9,6},... | collective-permute-start | bytes 178184 | tf_op jit(solution)/shard_map/ppermute | solution.py:58
  53.8 0.8 collective-permute-done.15
  54.6 4.2 %collective-permute-done.16 = bf16[58,512]{1,0:T(8,128)(2,1)S(1)} collective-permute-done((bf16[58,512]{1,0:T(8,128)(2,1)S(1)}, bf16[58,512]{1,0:T(8,128)(2,1)S(1)}, u32[]{:S(2)}, u32[]{:S(2)}) %collective-permute-start.16) | collective-permute-done | bytes 59424 | tf_op jit(solution)/shard_map/ppermute | solution.py:58
  58.8 0.6 gather_fusion.1
  59.4 0.3 reshape.426
  59.7 2.1 %gather_fusion.2 = bf16[384,512]{1,0:T(8,128)(2,1)S(1)} fusion(bf16[928,512]{1,0:T(8,128)(2,1)S(1)} %reshape.426, s32[1024]{0:T(1024)S(1)} %get-tuple-element.221), kind=kCustom, calls=%fused_computation.2 | custom fusion | bytes 787968 | tf_op jit(solution)/shard_map/gather | solution.py:126
  61.8 0.4 fusion.12
  62.2 34.5 %while.18 = (s32[]{:T(128)}, bf16[384,512]{1,0:T(8,128)(2,1)S(1)}, bf16[384,512]{1,0:T(8,128)(2,1)S(1)}, f32[384]{0:T(512)S(1)}, s32[384]{0:T(512)S(1)}, /*index...) while((s32[]{:T(128)}, bf16[384,512]{1,0:T(8,128)(2,1)S(1)}, ...), condition=%wide.region_26.27_spmd.clone, body=%wide.region_21.26_spmd.clone.sunk | while | flops 303321984 | bytes 6322649 | solution.py:147
  62.2 2.0 %collective-permute-start = (bf16[384,512]{1,0:T(8,128)(2,1)S(1)}, bf16[384,512]{1,0:T(8,128)(2,1)S(1)}, u32[]{:S(2)}, u32[]{:S(2)}) collective-permute-start(bf16[384,512]{1,0:T(8,128)(2,1)S(1)} %get-tuple-element.291), channel_id=1, source_target_pairs={{0,1},{1,2},{2,3},{3,4},{4,5},{5,6},{6,7},{7,8},{8,9},{9,10},{10,1... | collective-permute-start | bytes 1179656 | tf_op jit(solution)/shard_map/while/body/eval_jaxpr/ppermute | solution.py:28
  64.2 1.3 collective-permute-start.1
  65.7 2.2 %collective-permute-done.1 = bf16[384,512]{1,0:T(8,128)(2,1)S(1)} collective-permute-done((bf16[384,512]{1,0:T(8,128)(2,1)S(1)}, bf16[384,512]{1,0:T(8,128)(2,1)S(1)}, u32[]{:S(2)}, u32[]{:S(2)}) %collective-permute-start.1) | collective-permute-done | bytes 393248 | tf_op jit(solution)/shard_map/while/body/eval_jaxpr/ppermute | solution.py:28
  67.8 0.4 fusion.90
  68.3 0.4 fusion.91
  68.8 8.0 %collective-permute-start = (bf16[384,512]{1,0:T(8,128)(2,1)S(1)}, bf16[384,512]{1,0:T(8,128)(2,1)S(1)}, u32[]{:S(2)}, u32[]{:S(2)}) collective-permute-start(bf16[384,512]{1,0:T(8,128)(2,1)S(1)} %get-tuple-element.291), channel_id=1, source_target_pairs={{0,1},{1,2},{2,3},{3,4},{4,5},{5,6},{6,7},{7,8},{8,9},{9,10},{10,1... | collective-permute-start | bytes 1179656 | tf_op jit(solution)/shard_map/while/body/eval_jaxpr/ppermute | solution.py:28
  76.7 1.3 collective-permute-start.1
  78.2 2.2 %collective-permute-done.1 = bf16[384,512]{1,0:T(8,128)(2,1)S(1)} collective-permute-done((bf16[384,512]{1,0:T(8,128)(2,1)S(1)}, bf16[384,512]{1,0:T(8,128)(2,1)S(1)}, u32[]{:S(2)}, u32[]{:S(2)}) %collective-permute-start.1) | collective-permute-done | bytes 393248 | tf_op jit(solution)/shard_map/while/body/eval_jaxpr/ppermute | solution.py:28
  80.3 0.4 fusion.90
  80.8 0.4 fusion.91
  81.3 10.9 %collective-permute-start = (bf16[384,512]{1,0:T(8,128)(2,1)S(1)}, bf16[384,512]{1,0:T(8,128)(2,1)S(1)}, u32[]{:S(2)}, u32[]{:S(2)}) collective-permute-start(bf16[384,512]{1,0:T(8,128)(2,1)S(1)} %get-tuple-element.291), channel_id=1, source_target_pairs={{0,1},{1,2},{2,3},{3,4},{4,5},{5,6},{6,7},{7,8},{8,9},{9,10},{10,1... | collective-permute-start | bytes 1179656 | tf_op jit(solution)/shard_map/while/body/eval_jaxpr/ppermute | solution.py:28
  92.2 1.3 collective-permute-start.1
  93.7 2.2 %collective-permute-done.1 = bf16[384,512]{1,0:T(8,128)(2,1)S(1)} collective-permute-done((bf16[384,512]{1,0:T(8,128)(2,1)S(1)}, bf16[384,512]{1,0:T(8,128)(2,1)S(1)}, u32[]{:S(2)}, u32[]{:S(2)}) %collective-permute-start.1) | collective-permute-done | bytes 393248 | tf_op jit(solution)/shard_map/while/body/eval_jaxpr/ppermute | solution.py:28
  95.8 0.4 fusion.90
  96.3 0.4 fusion.91
  96.8 2.9 %scatter_custom_fusion.2 = f32[928]{0:T(1024)S(1)} fusion(s32[384]{0:T(512)S(1)} %fusion.58, f32[384]{0:T(512)S(1)} %get-tuple-element.141, f32[]{:T(128)} %constant.155.clone.1), kind=kCustom, calls=%fused_computation.163 | custom fusion | bytes 3716 | tf_op jit(solution)/shard_map/scatter | solution.py:150
  99.7 0.7 all_to_all.8
  100.4 13.4 %all-to-all-start = ((f32[16,58,1]{1,2,0:T(1,128)}), f32[16,58,1]{1,2,0:T(1,128)S(1)}, u32[]{:S(2)}, u32[]{:S(2)}) async-start(f32[16,58,1]{1,2,0:T(1,128)} %bitcast.40), calls=%async_computation | async-start | bytes 16384 | tf_op jit(solution)/shard_map/all_to_all | solution.py:152
  113.8 1.4 %fusion.13 = f32[384]{0:T(512)S(1)} fusion(bf16[384,512]{1,0:T(8,128)(2,1)S(1)} %fusion.15, f32[64,512]{1,0:T(8,128)} %all-reduce.2.cloned.1.call-done, s32[384]{0:T(512)S(1)} %copy-done.1), kind=kOutput, calls=%fused_computation.29 | convolution fusion | flops 151068288 | bytes 527360 | tf_op jit(solution)/shard_map/dot_general | solution.py:167
  115.2 5.0 %all-to-all-done = f32[16,58,1]{1,2,0:T(1,128)S(1)} async-done(((f32[16,58,1]{1,2,0:T(1,128)}), f32[16,58,1]{1,2,0:T(1,128)S(1)}, u32[]{:S(2)}, u32[]{:S(2)}) %all-to-all-start) | async-done | bytes 3744 | tf_op jit(solution)/shard_map/all_to_all | solution.py:152
  120.2 0.5 broadcast.584
  120.7 0.7 reduce.13
  121.5 1.9 %gather_fusion.3 = f32[384]{0:T(512)S(1)} fusion(f32[928]{0:T(1024)S(1)} %all_to_all.10, s32[1024]{0:T(1024)S(1)} %pad_clamp_fusion), kind=kCustom, calls=%fused_computation.3 | custom fusion | bytes 4608 | tf_op jit(solution)/shard_map/gather | solution.py:153
  123.4 0.6 convert_divide_fusion
  (93 shorter events, 2.2 us)
Async XLA Ops:
  7.2 1.3 copy-start
  7.2 106.6 %all-reduce.2.cloned.1.call-start = ((), (), s32[]{:S(2)}) async-start(), calls=%async_computation.1 | async-start | bytes 262144 | tf_op jit(solution)/shard_map/psum | solution.py:163
  8.4 0.7 copy-start.1
  10.0 0.7 copy-start.2
  24.6 5.1 %collective-permute-start.2 = (bf16[58,512]{1,0:T(8,128)(2,1)S(1)}, bf16[58,512]{1,0:T(8,128)(2,1)S(1)}, u32[]{:S(2)}, u32[]{:S(2)}) collective-permute-start(bf16[58,512]{1,0:T(8,128)(2,1)S(1)} %get-tuple-element.208), channel_id=1, source_target_pairs={{0,1},{1,0},{2,3},{3,2},{4,5},{5,4},{6,7},{7,6},{8,9},{9,8},{10,11... | collective-permute-start | bytes 178184 | tf_op jit(solution)/shard_map/ppermute | solution.py:58
  25.2 7.3 %collective-permute-start.3 = (bf16[58,512]{1,0:T(8,128)(2,1)S(1)}, bf16[58,512]{1,0:T(8,128)(2,1)S(1)}, u32[]{:S(2)}, u32[]{:S(2)}) collective-permute-start(bf16[58,512]{1,0:T(8,128)(2,1)S(1)} %get-tuple-element.207), channel_id=1, source_target_pairs={{0,2},{1,3},{2,0},{3,1},{4,6},{5,7},{6,4},{7,5},{8,10},{9,11},{10,... | collective-permute-start | bytes 178184 | tf_op jit(solution)/shard_map/ppermute | solution.py:58
  27.8 4.8 %collective-permute-start.4 = (bf16[58,512]{1,0:T(8,128)(2,1)S(1)}, bf16[58,512]{1,0:T(8,128)(2,1)S(1)}, u32[]{:S(2)}, u32[]{:S(2)}) collective-permute-start(bf16[58,512]{1,0:T(8,128)(2,1)S(1)} %get-tuple-element.206), channel_id=1, source_target_pairs={{0,3},{1,2},{2,1},{3,0},{4,7},{5,6},{6,5},{7,4},{8,11},{9,10},{10,... | collective-permute-start | bytes 178184 | tf_op jit(solution)/shard_map/ppermute | solution.py:58
  27.8 7.5 %collective-permute-start.5 = (bf16[58,512]{1,0:T(8,128)(2,1)S(1)}, bf16[58,512]{1,0:T(8,128)(2,1)S(1)}, u32[]{:S(2)}, u32[]{:S(2)}) collective-permute-start(bf16[58,512]{1,0:T(8,128)(2,1)S(1)} %get-tuple-element.205), channel_id=1, source_target_pairs={{0,4},{1,5},{2,6},{3,7},{4,0},{5,1},{6,2},{7,3},{8,12},{9,13},{10,... | collective-permute-start | bytes 178184 | tf_op jit(solution)/shard_map/ppermute | solution.py:58
  29.6 6.7 %collective-permute-start.6 = (bf16[58,512]{1,0:T(8,128)(2,1)S(1)}, bf16[58,512]{1,0:T(8,128)(2,1)S(1)}, u32[]{:S(2)}, u32[]{:S(2)}) collective-permute-start(bf16[58,512]{1,0:T(8,128)(2,1)S(1)} %get-tuple-element.204), channel_id=1, source_target_pairs={{0,5},{1,4},{2,7},{3,6},{4,1},{5,0},{6,3},{7,2},{8,13},{9,12},{10,... | collective-permute-start | bytes 178184 | tf_op jit(solution)/shard_map/ppermute | solution.py:58
  29.7 9.3 %collective-permute-start.7 = (bf16[58,512]{1,0:T(8,128)(2,1)S(1)}, bf16[58,512]{1,0:T(8,128)(2,1)S(1)}, u32[]{:S(2)}, u32[]{:S(2)}) collective-permute-start(bf16[58,512]{1,0:T(8,128)(2,1)S(1)} %get-tuple-element.203), channel_id=1, source_target_pairs={{0,6},{1,7},{2,4},{3,5},{4,2},{5,3},{6,0},{7,1},{8,14},{9,15},{10,... | collective-permute-start | bytes 178184 | tf_op jit(solution)/shard_map/ppermute | solution.py:58
  32.5 7.3 %collective-permute-start.8 = (bf16[58,512]{1,0:T(8,128)(2,1)S(1)}, bf16[58,512]{1,0:T(8,128)(2,1)S(1)}, u32[]{:S(2)}, u32[]{:S(2)}) collective-permute-start(bf16[58,512]{1,0:T(8,128)(2,1)S(1)} %get-tuple-element.202), channel_id=1, source_target_pairs={{0,7},{1,6},{2,5},{3,4},{4,3},{5,2},{6,1},{7,0},{8,15},{9,14},{10,... | collective-permute-start | bytes 178184 | tf_op jit(solution)/shard_map/ppermute | solution.py:58
  32.6 10.3 %collective-permute-start.9 = (bf16[58,512]{1,0:T(8,128)(2,1)S(1)}, bf16[58,512]{1,0:T(8,128)(2,1)S(1)}, u32[]{:S(2)}, u32[]{:S(2)}) collective-permute-start(bf16[58,512]{1,0:T(8,128)(2,1)S(1)} %get-tuple-element.201), channel_id=1, source_target_pairs={{0,8},{1,9},{2,10},{3,11},{4,12},{5,13},{6,14},{7,15},{8,0},{9,1},... | collective-permute-start | bytes 178184 | tf_op jit(solution)/shard_map/ppermute | solution.py:58
  35.4 12.1 %collective-permute-start.10 = (bf16[58,512]{1,0:T(8,128)(2,1)S(1)}, bf16[58,512]{1,0:T(8,128)(2,1)S(1)}, u32[]{:S(2)}, u32[]{:S(2)}) collective-permute-start(bf16[58,512]{1,0:T(8,128)(2,1)S(1)} %get-tuple-element.200), channel_id=1, source_target_pairs={{0,9},{1,8},{2,11},{3,10},{4,13},{5,12},{6,15},{7,14},{8,1},{9,0},... | collective-permute-start | bytes 178184 | tf_op jit(solution)/shard_map/ppermute | solution.py:58
  36.3 15.3 %collective-permute-start.11 = (bf16[58,512]{1,0:T(8,128)(2,1)S(1)}, bf16[58,512]{1,0:T(8,128)(2,1)S(1)}, u32[]{:S(2)}, u32[]{:S(2)}) collective-permute-start(bf16[58,512]{1,0:T(8,128)(2,1)S(1)} %get-tuple-element.199), channel_id=1, source_target_pairs={{0,10},{1,11},{2,8},{3,9},{4,14},{5,15},{6,12},{7,13},{8,2},{9,3},... | collective-permute-start | bytes 178184 | tf_op jit(solution)/shard_map/ppermute | solution.py:58
  39.1 14.6 %collective-permute-start.12 = (bf16[58,512]{1,0:T(8,128)(2,1)S(1)}, bf16[58,512]{1,0:T(8,128)(2,1)S(1)}, u32[]{:S(2)}, u32[]{:S(2)}) collective-permute-start(bf16[58,512]{1,0:T(8,128)(2,1)S(1)} %get-tuple-element.198), channel_id=1, source_target_pairs={{0,11},{1,10},{2,9},{3,8},{4,15},{5,14},{6,13},{7,12},{8,3},{9,2},... | collective-permute-start | bytes 178184 | tf_op jit(solution)/shard_map/ppermute | solution.py:58
  39.7 14.0 %collective-permute-start.13 = (bf16[58,512]{1,0:T(8,128)(2,1)S(1)}, bf16[58,512]{1,0:T(8,128)(2,1)S(1)}, u32[]{:S(2)}, u32[]{:S(2)}) collective-permute-start(bf16[58,512]{1,0:T(8,128)(2,1)S(1)} %get-tuple-element.197), channel_id=1, source_target_pairs={{0,12},{1,13},{2,14},{3,15},{4,8},{5,9},{6,10},{7,11},{8,4},{9,5},... | collective-permute-start | bytes 178184 | tf_op jit(solution)/shard_map/ppermute | solution.py:58
  42.9 10.9 %collective-permute-start.14 = (bf16[58,512]{1,0:T(8,128)(2,1)S(1)}, bf16[58,512]{1,0:T(8,128)(2,1)S(1)}, u32[]{:S(2)}, u32[]{:S(2)}) collective-permute-start(bf16[58,512]{1,0:T(8,128)(2,1)S(1)} %get-tuple-element.196), channel_id=1, source_target_pairs={{0,13},{1,12},{2,15},{3,14},{4,9},{5,8},{6,11},{7,10},{8,5},{9,4},... | collective-permute-start | bytes 178184 | tf_op jit(solution)/shard_map/ppermute | solution.py:58
  47.5 7.1 %collective-permute-start.15 = (bf16[58,512]{1,0:T(8,128)(2,1)S(1)}, bf16[58,512]{1,0:T(8,128)(2,1)S(1)}, u32[]{:S(2)}, u32[]{:S(2)}) collective-permute-start(bf16[58,512]{1,0:T(8,128)(2,1)S(1)} %get-tuple-element.195), channel_id=1, source_target_pairs={{0,14},{1,15},{2,12},{3,13},{4,10},{5,11},{6,8},{7,9},{8,6},{9,7},... | collective-permute-start | bytes 178184 | tf_op jit(solution)/shard_map/ppermute | solution.py:58
  51.6 7.2 %collective-permute-start.16 = (bf16[58,512]{1,0:T(8,128)(2,1)S(1)}, bf16[58,512]{1,0:T(8,128)(2,1)S(1)}, u32[]{:S(2)}, u32[]{:S(2)}) collective-permute-start(bf16[58,512]{1,0:T(8,128)(2,1)S(1)} %get-tuple-element.194), channel_id=1, source_target_pairs={{0,15},{1,14},{2,13},{3,12},{4,11},{5,10},{6,9},{7,8},{8,7},{9,6},... | collective-permute-start | bytes 178184 | tf_op jit(solution)/shard_map/ppermute | solution.py:58
  62.2 6.0 %collective-permute-start = (bf16[384,512]{1,0:T(8,128)(2,1)S(1)}, bf16[384,512]{1,0:T(8,128)(2,1)S(1)}, u32[]{:S(2)}, u32[]{:S(2)}) collective-permute-start(bf16[384,512]{1,0:T(8,128)(2,1)S(1)} %get-tuple-element.291), channel_id=1, source_target_pairs={{0,1},{1,2},{2,3},{3,4},{4,5},{5,6},{6,7},{7,8},{8,9},{9,10},{10,1... | collective-permute-start | bytes 1179656 | tf_op jit(solution)/shard_map/while/body/eval_jaxpr/ppermute | solution.py:28
  64.2 3.6 %collective-permute-start.1 = (bf16[384,512]{1,0:T(8,128)(2,1)S(1)}, bf16[384,512]{1,0:T(8,128)(2,1)S(1)}, u32[]{:S(2)}, u32[]{:S(2)}) collective-permute-start(bf16[384,512]{1,0:T(8,128)(2,1)S(1)} %get-tuple-element.292), channel_id=1, source_target_pairs={{1,0},{2,1},{3,2},{4,3},{5,4},{6,5},{7,6},{8,7},{9,8},{10,9},{11,1... | collective-permute-start | bytes 1179656 | tf_op jit(solution)/shard_map/while/body/eval_jaxpr/ppermute | solution.py:28
  68.8 12.0 %collective-permute-start = (bf16[384,512]{1,0:T(8,128)(2,1)S(1)}, bf16[384,512]{1,0:T(8,128)(2,1)S(1)}, u32[]{:S(2)}, u32[]{:S(2)}) collective-permute-start(bf16[384,512]{1,0:T(8,128)(2,1)S(1)} %get-tuple-element.291), channel_id=1, source_target_pairs={{0,1},{1,2},{2,3},{3,4},{4,5},{5,6},{6,7},{7,8},{8,9},{9,10},{10,1... | collective-permute-start | bytes 1179656 | tf_op jit(solution)/shard_map/while/body/eval_jaxpr/ppermute | solution.py:28
  76.7 3.6 %collective-permute-start.1 = (bf16[384,512]{1,0:T(8,128)(2,1)S(1)}, bf16[384,512]{1,0:T(8,128)(2,1)S(1)}, u32[]{:S(2)}, u32[]{:S(2)}) collective-permute-start(bf16[384,512]{1,0:T(8,128)(2,1)S(1)} %get-tuple-element.292), channel_id=1, source_target_pairs={{1,0},{2,1},{3,2},{4,3},{5,4},{6,5},{7,6},{8,7},{9,8},{10,9},{11,1... | collective-permute-start | bytes 1179656 | tf_op jit(solution)/shard_map/while/body/eval_jaxpr/ppermute | solution.py:28
  81.3 15.0 %collective-permute-start = (bf16[384,512]{1,0:T(8,128)(2,1)S(1)}, bf16[384,512]{1,0:T(8,128)(2,1)S(1)}, u32[]{:S(2)}, u32[]{:S(2)}) collective-permute-start(bf16[384,512]{1,0:T(8,128)(2,1)S(1)} %get-tuple-element.291), channel_id=1, source_target_pairs={{0,1},{1,2},{2,3},{3,4},{4,5},{5,6},{6,7},{7,8},{8,9},{9,10},{10,1... | collective-permute-start | bytes 1179656 | tf_op jit(solution)/shard_map/while/body/eval_jaxpr/ppermute | solution.py:28
  92.2 3.6 %collective-permute-start.1 = (bf16[384,512]{1,0:T(8,128)(2,1)S(1)}, bf16[384,512]{1,0:T(8,128)(2,1)S(1)}, u32[]{:S(2)}, u32[]{:S(2)}) collective-permute-start(bf16[384,512]{1,0:T(8,128)(2,1)S(1)} %get-tuple-element.292), channel_id=1, source_target_pairs={{1,0},{2,1},{3,2},{4,3},{5,4},{6,5},{7,6},{8,7},{9,8},{10,9},{11,1... | collective-permute-start | bytes 1179656 | tf_op jit(solution)/shard_map/while/body/eval_jaxpr/ppermute | solution.py:28
  100.4 19.8 %all-to-all-start = ((f32[16,58,1]{1,2,0:T(1,128)}), f32[16,58,1]{1,2,0:T(1,128)S(1)}, u32[]{:S(2)}, u32[]{:S(2)}) async-start(f32[16,58,1]{1,2,0:T(1,128)} %bitcast.40), calls=%async_computation | async-start | bytes 16384 | tf_op jit(solution)/shard_map/all_to_all | solution.py:152
Sparse Core Ops, SparseCore 0:
  11.4 97.3 all-reduce.1
